TPU v7x, 32 devices: a whole 2x2x4 slice. The times are simulated.
32 devices in a mesh: tok: 8 (over z, x), exp: 4 (over y, core).
Axes of the slice: x: 2, y: 2, z: 4, core: 2. Of those that a mesh axis runs over, the one named last changes fastest.
Arguments:
- tokens: bfloat16 [16384, 7168], P('tok', 'exp'), may hold values from -6 to 6
- gate_weight: bfloat16 [7168, 256], P('exp'), may hold values from -0.0625 to 0.0625
- expert_ids: int32 [16384, 8], P('tok'), may hold values from 0 to 255, all different within a row
- expert_bias: float32 [256], P('exp'), may hold values from -0.002 to 0.002
Outputs:
- affinities: float32 [16384, 256], P('tok', 'exp')
- weights: float32 [16384, 8], P('tok')
- load: float32 [256], replicated
- new_bias: float32 [256], replicated
All inputs are finite; a program needn't handle non-finite values.
Results may differ from a plain program's by a relative error of at most 0.0003.
Values may be sent and summed in bfloat16 or wider, within the bound.
No kernel may reach another device: no remote copies, remote signals or barrier semaphores. Data moves between devices by JAX's collectives and lax.ppermute only.
A program may use at most 64 MiB of HBM per device.

v0:
```python
import jax
import jax.numpy as jnp
from jax import lax
from jax.sharding import PartitionSpec as P


def count_experts(expert_ids, width):
    numbers = lax.iota(jnp.int32, width)
    matches = expert_ids[:, :, None] == numbers[None, None, :]
    return jnp.sum(matches.astype(jnp.float32), axis=(0, 1))


def local(tokens, gate_weight, expert_ids, expert_bias):
    experts_all = gate_weight.shape[1]
    own_width = expert_bias.shape[0]
    first_expert = lax.axis_index("exp") * own_width
    tok_rows = tokens.shape[0]
    partial_logits = jnp.dot(tokens, gate_weight, preferred_element_type=jnp.float32)
    logits = lax.psum_scatter(partial_logits, "exp", scatter_dimension=1, tiled=True)
    affinities = jax.nn.sigmoid(logits)
    numbers = first_expert + lax.iota(jnp.int32, own_width)
    matches = expert_ids[:, :, None] == numbers[None, None, :]
    chosen_part = jnp.sum(jnp.where(matches, affinities[:, None, :], jnp.float32(0.0)), axis=2)
    chosen = lax.psum(chosen_part, "exp")
    weights = 2.5 * chosen / jnp.sum(chosen, axis=1, keepdims=True)
    target = jnp.float32(tok_rows * lax.axis_size("tok") * expert_ids.shape[1])
    bias_whole = lax.all_gather(expert_bias, "exp", axis=0, tiled=True)
    load = lax.psum(count_experts(expert_ids, experts_all), "tok")
    new_bias = bias_whole + 0.001 * jnp.sign(target - jnp.float32(experts_all) * load)
    return (affinities, weights, load, new_bias)


def solution(mesh):
    in_specs = (P("tok", "exp"), P("exp", None), P("tok", None), P("exp"))
    out_specs = (P("tok", "exp"), P("tok", None), P(), P())
    return jax.shard_map(local, mesh=mesh, in_specs=in_specs, out_specs=out_specs, check_vma=False)
```

profile of v0, /device:TPU:0, one launch (start us, length us, event | category | flops | bytes accessed | tf_op | source)
XLA Modules:
  0.0 92.7 jit_solution(2102868022089184914)
XLA Ops:
  7.2 0.0 copy-start
  7.2 0.0 copy-start.5
  7.2 0.0 copy-start.2
  7.2 0.0 copy-start.4
  7.2 0.0 reduce-scatter.2.cloned.1.call-start
  7.3 1.1 %copy-done = bf16[1792,256]{1,0:T(8,128)(2,1)S(1)} copy-done((bf16[1792,256]{1,0:T(8,128)(2,1)S(1)}, bf16[1792,256]{1,0:T(8,128)(2,1)}, u32[]{:S(2)}) %copy-start) | copy-done | bytes 917528
  8.4 6.5 %fusion = f32[2048,256]{0,1:T(8,128)} fusion(bf16[2048,1792]{1,0:T(8,128)(2,1)} %param.4, bf16[1792,256]{1,0:T(8,128)(2,1)S(1)} %copy-done), kind=kOutput, calls=%fused_computation.7 | convolution fusion | flops 1879048192 | bytes 10354688 | tf_op jit(solution)/shard_map/dot_general | solution.py:18
  14.9 0.0 reduce-scatter.2.cloned.1.call-update
  14.9 0.0 all-reduce.3.cloned.1.call-start
  15.0 0.0 copy-done.2
  15.0 0.3 copy.11
  15.4 0.0 copy-done.5
  15.4 0.6 dynamic-slice
  16.6 0.0 copy-done.4
  16.6 0.2 dynamic-update-slice
  16.9 5.1 %convert_reduce_fusion = f32[256]{0:T(256)S(1)} fusion(s32[2048,8]{1,0:T(8,128)S(1)} %copy.11), kind=kLoop, calls=%fused_computation | loop fusion | flops 12582656 | bytes 66560 | tf_op jit(solution)/shard_map/reduce_sum | solution.py:10
  22.0 23.1 %psum.15 = f32[256]{0:T(256)S(1)} all-reduce(f32[256]{0:T(256)S(1)} %convert_reduce_fusion), channel_id=1, replica_groups=mesh['tok'=8,'exp'=4] {'tok'}, use_global_device_ids=true, to_apply=%region_5.6 | all-reduce | flops 256 | bytes 2048 | tf_op jit(solution)/shard_map/psum | solution.py:28
  45.1 0.0 copy-start.3
  45.1 5.7 %all-reduce = f32[256]{0:T(256)S(1)} all-reduce(f32[256]{0:T(256)S(1)} %dynamic-update-slice), channel_id=1, replica_groups=mesh['tok'=8,'exp'=4] {'exp'}, use_global_device_ids=true, to_apply=%add | all-reduce | flops 256 | bytes 2048
  50.8 0.0 reduce-scatter.2.cloned.1.call-done
  50.8 1.2 %add_divide_fusion = f32[2048,64]{0,1:T(8,128)S(1)} fusion(f32[2048,64]{0,1:T(8,128)} %reduce-scatter.2.cloned.1.call-done), kind=kLoop, calls=%fused_computation.3 | loop fusion | flops 393216 | bytes 1048576 | tf_op jit(solution)/shard_map/div | solution.py:20
  52.0 0.0 copy-start.1
  52.0 1.2 %select_reduce_fusion = f32[2048,8]{0,1:T(8,128)} fusion(f32[2048,64]{0,1:T(8,128)S(1)} %add_divide_fusion, s32[2048,8]{0,1:T(8,128)S(1)} %copy-done.2, s32[64]{0:T(128)S(1)} %iota_add_fusion), kind=kLoop, calls=%fused_computation.2 | loop fusion | flops 3129344 | bytes 655616 | tf_op jit(solution)/shard_map/reduce_sum | solution.py:23
  53.2 0.0 all-reduce.3.cloned.1.call-update
  53.2 0.6 multiply_add_fusion
  53.8 29.7 %all-reduce.3.cloned.1.call-done = f32[2048,8]{0,1:T(8,128)} async-done(((f32[2048,8]{0,1:T(8,128)}), f32[2048,8]{0,1:T(8,128)}) %all-reduce.3.cloned.1.call-update) | async-done | bytes 65552 | tf_op jit(solution)/shard_map/psum | solution.py:24
  83.5 0.9 reduce_sum.28
  84.4 1.5 %multiply_divide_fusion = f32[2048,8]{0,1:T(8,128)} fusion(f32[2048,8]{0,1:T(8,128)} %all-reduce.3.cloned.1.call-done, f32[2048]{0:T(1024)S(1)} %reduce_sum.28), kind=kLoop, calls=%fused_computation.4 | loop fusion | flops 32768 | bytes 139264 | tf_op jit(solution)/shard_map/div | solution.py:25
  85.9 0.0 copy-done.3
  85.9 0.0 copy-done.1
  (2 shorter events, 0.0 us)
Async XLA Ops:
  7.2 1.2 %copy-start = (bf16[1792,256]{1,0:T(8,128)(2,1)S(1)}, bf16[1792,256]{1,0:T(8,128)(2,1)}, u32[]{:S(2)}) copy-start(bf16[1792,256]{1,0:T(8,128)(2,1)} %param.5) | copy-start | bytes 2752516
  7.2 8.2 %copy-start.5 = (u32[32]{0:T(128)S(1)}, u32[32]{0:T(128)}, u32[]{:S(2)}) copy-start(u32[32]{0:T(128)} %constant.20) | copy-start | bytes 388
  7.2 7.8 %copy-start.2 = (s32[2048,8]{0,1:T(8,128)S(1)}, s32[2048,8]{0,1:T(8,128)}, u32[]{:S(2)}) copy-start(s32[2048,8]{0,1:T(8,128)} %param.6) | copy-start | bytes 196612
  7.2 9.4 %copy-start.4 = (f32[64]{0:T(128)S(1)}, f32[64]{0:T(128)}, u32[]{:S(2)}) copy-start(f32[64]{0:T(128)} %param.7) | copy-start | bytes 772
  7.2 43.6 %reduce-scatter.2.cloned.1.call-start = ((), (), s32[]{:S(2)}) async-start(), calls=%async_computation.1 | async-start | bytes 2621440 | tf_op jit(solution)/shard_map/reduce_scatter | solution.py:19
  14.9 68.6 %all-reduce.3.cloned.1.call-start = ((), (), s32[]{:S(2)}) async-start(), calls=%async_computation.2 | async-start | bytes 131072 | tf_op jit(solution)/shard_map/psum | solution.py:24
  45.1 40.8 %copy-start.3 = (f32[256]{0:T(256)}, f32[256]{0:T(256)S(1)}, u32[]{:S(2)}) copy-start(f32[256]{0:T(256)S(1)} %psum.15) | copy-start | bytes 3076
  52.0 33.9 %copy-start.1 = (f32[2048,64]{0,1:T(8,128)}, f32[2048,64]{0,1:T(8,128)S(1)}, u32[]{:S(2)}) copy-start(f32[2048,64]{0,1:T(8,128)S(1)} %add_divide_fusion) | copy-start | bytes 1572868
Sparse Core Ops, SparseCore 0:
  15.1 33.8 reduce-scatter.1
  53.3 30.1 all-reduce.2
where the time goes:
time: 93.1 us; the launch traced here: 92.7 us
  waiting for transfers between devices  29.8 us (32%)
  blocking collectives  28.8 us (31%)
  between operations  14.8 us (16%)
  other arithmetic  10.4 us (11%)
  matrix products  6.53 us (7%)
  local copies, waits for them, and re-layouts  2.31 us (2%)
    psum x1, waiting for transfers between devices, local(): chosen = lax.psum(chosen_part, 'exp')  29.7 us
    psum x1, blocking collectives, local(): load = lax.psum(count_experts(expert_ids, experts_all), 'tok')  23.1 us
    dot_general x1, matrix products, local(): jnp.dot(tokens, gate_weight, preferred_element_type=jnp.float32)  6.53 us
    unnamed x1, blocking collectives  5.66 us
    reduce_sum x1, other arithmetic, count_experts(): return jnp.sum(matches.astype(jnp.float32), axis=(0, 1))  5.11 us
    unnamed x16, local copies, waits for them, and re-layouts  2.31 us
  transfers between devices with their start and end apart: 2, of which 1 were waited for; matrix products, arithmetic and copies ran while one was open for 7% of the time, Pallas kernels for 0%

commit v1 on v0

--- a/solution.py
+++ b/solution.py
@@ -2,6 +2,14 @@
 import jax.numpy as jnp
 from jax import lax
 from jax.sharding import PartitionSpec as P
+
+
+def doubling_sum(array, axis):
+    size, result = (lax.axis_size(axis), array)
+    for far in [1 << k for k in range(size.bit_length() - 1)]:
+        route = [(i, i ^ far) for i in range(size)]
+        result = result + lax.ppermute(result, axis, route)
+    return result
 
 
 def count_experts(expert_ids, width):
@@ -21,7 +29,7 @@
     numbers = first_expert + lax.iota(jnp.int32, own_width)
     matches = expert_ids[:, :, None] == numbers[None, None, :]
     chosen_part = jnp.sum(jnp.where(matches, affinities[:, None, :], jnp.float32(0.0)), axis=2)
-    chosen = lax.psum(chosen_part, "exp")
+    chosen = doubling_sum(chosen_part, "exp")
     weights = 2.5 * chosen / jnp.sum(chosen, axis=1, keepdims=True)
     target = jnp.float32(tok_rows * lax.axis_size("tok") * expert_ids.shape[1])
     bias_whole = lax.all_gather(expert_bias, "exp", axis=0, tiled=True)

time: 93.1 us -> 96.9 us (1.041)
  waiting for transfers between devices: 29.8 us -> 37.2 us
  other arithmetic: 10.4 us -> 8.14 us
  blocking collectives: 28.8 us -> 27.3 us
    reduce_scatter x1, waiting for transfers between devices: 0.01 us -> 33.7 us  [local(): lax.psum_scatter(partial_logits, 'exp', scatter_dimension=1, tiled=True)]
    psum x1 -> x0, waiting for transfers between devices: 29.7 us -> none  [local(): chosen = lax.psum(chosen_part, 'exp')]
    ppermute x0 -> x2, waiting for transfers between devices: none -> 3.42 us  [doubling_sum(): result = result + lax.ppermute(result, axis, route)]
    psum x1, blocking collectives: 23.1 us -> 21.3 us  [local(): load = lax.psum(count_experts(expert_ids, experts_all), 'tok')]
  transfers between devices with their start and end apart: 2 -> 3, of which waited for: 1 -> 2; matrix products, arithmetic and copies ran while one was open for 7% -> 7% of each run, Pallas kernels for 0% -> 0%
where the time goes in v1:
time: 96.9 us; the launch traced here: 96.6 us
  waiting for transfers between devices  37.2 us (38%)
  blocking collectives  27.3 us (28%)
  between operations  14.8 us (15%)
  other arithmetic  8.14 us (8%)
  matrix products  6.54 us (7%)
  local copies, waits for them, and re-layouts  2.3 us (2%)
    reduce_scatter x1, waiting for transfers between devices, local(): lax.psum_scatter(partial_logits, 'exp', scatter_dimension=1, tiled=True)  33.7 us
    psum x1, blocking collectives, local(): load = lax.psum(count_experts(expert_ids, experts_all), 'tok')  21.3 us
    dot_general x1, matrix products, local(): jnp.dot(tokens, gate_weight, preferred_element_type=jnp.float32)  6.54 us
    unnamed x1, blocking collectives  5.96 us
    reduce_sum x1, other arithmetic, count_experts(): return jnp.sum(matches.astype(jnp.float32), axis=(0, 1))  5.12 us
    ppermute x2, waiting for transfers between devices, doubling_sum(): result = result + lax.ppermute(result, axis, route)  3.42 us
    unnamed x16, local copies, waits for them, and re-layouts  2.3 us
  transfers between devices with their start and end apart: 3, of which 2 were waited for; matrix products, arithmetic and copies ran while one was open for 7% of the time, Pallas kernels for 0%

profile of v1, /device:TPU:0, one launch (start us, length us, event | category | flops | bytes accessed | tf_op | source)
XLA Modules:
  0.0 96.6 jit_solution(599852570344160764)
XLA Ops:
  7.2 0.0 copy-start
  7.2 0.0 copy-start.2
  7.2 0.0 reduce-scatter.2.cloned.1.call-start
  7.2 1.1 %copy-done = bf16[1792,256]{1,0:T(8,128)(2,1)S(1)} copy-done((bf16[1792,256]{1,0:T(8,128)(2,1)S(1)}, bf16[1792,256]{1,0:T(8,128)(2,1)}, u32[]{:S(2)}) %copy-start) | copy-done | bytes 917528
  8.4 6.5 %fusion = f32[2048,256]{0,1:T(8,128)} fusion(bf16[2048,1792]{1,0:T(8,128)(2,1)} %param.4, bf16[1792,256]{1,0:T(8,128)(2,1)S(1)} %copy-done), kind=kOutput, calls=%fused_computation.8 | convolution fusion | flops 1879048192 | bytes 10354688 | tf_op jit(solution)/shard_map/dot_general | solution.py:26
  14.9 0.0 copy-start.5
  14.9 0.0 copy-start.4
  14.9 0.0 reduce-scatter.2.cloned.1.call-update
  14.9 0.0 copy-done.2
  14.9 0.3 copy.11
  15.3 33.7 %reduce-scatter.2.cloned.1.call-done = f32[2048,64]{0,1:T(8,128)} async-done(((f32[2048,256]{0,1:T(8,128)}), f32[2048,64]{0,1:T(8,128)}) %reduce-scatter.2.cloned.1.call-update) | async-done | bytes 524304 | tf_op jit(solution)/shard_map/reduce_scatter | solution.py:27
  49.0 1.2 %add_divide_fusion = f32[2048,64]{0,1:T(8,128)S(1)} fusion(f32[2048,64]{0,1:T(8,128)} %reduce-scatter.2.cloned.1.call-done), kind=kLoop, calls=%fused_computation.3 | loop fusion | flops 393216 | bytes 1048576 | tf_op jit(solution)/shard_map/div | solution.py:28
  50.2 0.0 copy-start.1
  50.2 0.6 select_reduce_fusion
  50.8 0.1 collective-permute-start
  50.9 5.1 %convert_reduce_fusion = f32[256]{0:T(256)S(1)} fusion(s32[2048,8]{1,0:T(8,128)S(1)} %copy.11), kind=kLoop, calls=%fused_computation | loop fusion | flops 12582656 | bytes 66560 | tf_op jit(solution)/shard_map/reduce_sum | solution.py:18
  56.0 0.0 copy-done.5
  56.0 0.6 dynamic-slice
  57.2 0.0 copy-done.4
  57.3 0.2 dynamic-update-slice
  57.5 21.3 %psum.7 = f32[256]{0:T(256)S(1)} all-reduce(f32[256]{0:T(256)S(1)} %convert_reduce_fusion), channel_id=1, replica_groups=mesh['tok'=8,'exp'=4] {'tok'}, use_global_device_ids=true, to_apply=%region_4.5 | all-reduce | flops 256 | bytes 2048 | tf_op jit(solution)/shard_map/psum | solution.py:36
  78.8 0.0 copy-start.3
  78.8 6.0 %all-reduce = f32[256]{0:T(256)S(1)} all-reduce(f32[256]{0:T(256)S(1)} %dynamic-update-slice), channel_id=1, replica_groups=mesh['tok'=8,'exp'=4] {'exp'}, use_global_device_ids=true, to_apply=%add | all-reduce | flops 256 | bytes 2048
  84.8 0.0 collective-permute-done
  84.8 0.3 collective-permute-start.1
  85.1 0.6 multiply_add_fusion
  85.7 3.4 %collective-permute-done.1 = f32[2048,8]{0,1:T(8,128)S(1)} collective-permute-done((f32[2048,8]{0,1:T(8,128)S(1)}, f32[2048,8]{0,1:T(8,128)S(1)}, u32[]{:S(2)}, u32[]{:S(2)}) %collective-permute-start.1) | collective-permute-done | bytes 65568 | tf_op jit(solution)/shard_map/ppermute | solution.py:11
  89.1 0.7 multiply_divide_fusion
  89.8 0.0 copy-done.1
  89.8 0.0 copy-done.3
  (4 shorter events, 0.0 us)
Async XLA Ops:
  7.2 1.2 %copy-start = (bf16[1792,256]{1,0:T(8,128)(2,1)S(1)}, bf16[1792,256]{1,0:T(8,128)(2,1)}, u32[]{:S(2)}) copy-start(bf16[1792,256]{1,0:T(8,128)(2,1)} %param.5) | copy-start | bytes 2752516
  7.2 7.7 %copy-start.2 = (s32[2048,8]{0,1:T(8,128)S(1)}, s32[2048,8]{0,1:T(8,128)}, u32[]{:S(2)}) copy-start(s32[2048,8]{0,1:T(8,128)} %param.6) | copy-start | bytes 196612
  7.2 41.8 %reduce-scatter.2.cloned.1.call-start = ((), (), s32[]{:S(2)}) async-start(), calls=%async_computation.1 | async-start | bytes 2621440 | tf_op jit(solution)/shard_map/reduce_scatter | solution.py:27
  14.9 41.1 %copy-start.5 = (u32[32]{0:T(128)S(1)}, u32[32]{0:T(128)}, u32[]{:S(2)}) copy-start(u32[32]{0:T(128)} %constant.20) | copy-start | bytes 388
  14.9 42.4 %copy-start.4 = (f32[64]{0:T(128)S(1)}, f32[64]{0:T(128)}, u32[]{:S(2)}) copy-start(f32[64]{0:T(128)} %param.7) | copy-start | bytes 772
  50.2 39.6 %copy-start.1 = (f32[2048,64]{0,1:T(8,128)}, f32[2048,64]{0,1:T(8,128)S(1)}, u32[]{:S(2)}) copy-start(f32[2048,64]{0,1:T(8,128)S(1)} %add_divide_fusion) | copy-start | bytes 1572868
  50.8 34.0 %collective-permute-start = (f32[2048,8]{0,1:T(8,128)S(1)}, f32[2048,8]{0,1:T(8,128)S(1)}, u32[]{:S(2)}, u32[]{:S(2)}) collective-permute-start(f32[2048,8]{0,1:T(8,128)S(1)} %select_reduce_fusion), channel_id=1, source_target_pairs={{0,1},{1,0},{2,3},{3,2},{4,5},{5,4},{6,7},{7,6},{8,9},{9,8},{10,11... | collective-permute-start | bytes 196616 | tf_op jit(solution)/shard_map/ppermute | solution.py:11
  78.8 11.0 %copy-start.3 = (f32[256]{0:T(256)}, f32[256]{0:T(256)S(1)}, u32[]{:S(2)}) copy-start(f32[256]{0:T(256)S(1)} %psum.7) | copy-start | bytes 3076
  84.8 4.3 %collective-permute-start.1 = (f32[2048,8]{0,1:T(8,128)S(1)}, f32[2048,8]{0,1:T(8,128)S(1)}, u32[]{:S(2)}, u32[]{:S(2)}) collective-permute-start(f32[2048,8]{0,1:T(8,128)S(1)} %add.29), channel_id=1, source_target_pairs={{0,2},{1,3},{2,0},{3,1},{4,6},{5,7},{6,4},{7,5},{8,10},{9,11},{10,... | collective-permute-start | bytes 196616 | tf_op jit(solution)/shard_map/ppermute | solution.py:11
Sparse Core Ops, SparseCore 0:
  15.0 33.9 reduce-scatter.1
